TPU v7x, 32 devices: a whole 2x2x4 slice. The times are simulated.
32 devices in a mesh: replica: 8 (over z, y), model: 4 (over x, core).
Axes of the slice: x: 2, y: 2, z: 4, core: 2. Of those that a mesh axis runs over, the one named last changes fastest.
Arguments:
- slope_up: float32 [8, 1024, 4096], P('replica', None, 'model'), may hold values from -4 to 4
- slope_down: float32 [8, 4096, 1024], P('replica', 'model'), may hold values from -4 to 4
- slope_query: float32 [8, 1024, 1024], P('replica', None, 'model'), may hold values from -4 to 4
- slope_key: float32 [8, 1024, 1024], P('replica', None, 'model'), may hold values from -4 to 4
- slope_value: float32 [8, 1024, 1024], P('replica', None, 'model'), may hold values from -4 to 4
- slope_mixed: float32 [8, 1024, 1024], P('replica', 'model'), may hold values from -4 to 4
- slope_norm: float32 [8, 1024], P('replica'), may hold values from -8 to 8
- slope_bias: float32 [8, 1024], P('replica'), may hold values from -8 to 8
- param_up: float32 [1024, 4096], P('replica', 'model'), may hold values from -0.25 to 0.25
- param_down: float32 [4096, 1024], P('model', 'replica'), may hold values from -0.125 to 0.125
- param_query: float32 [1024, 1024], P('replica', 'model'), may hold values from -0.25 to 0.25
- param_key: float32 [1024, 1024], P('replica', 'model'), may hold values from -0.25 to 0.25
- param_value: float32 [1024, 1024], P('replica', 'model'), may hold values from -0.25 to 0.25
- param_mixed: float32 [1024, 1024], P('model', 'replica'), may hold values from -0.25 to 0.25
- param_norm: float32 [1024], P('replica'), may hold values from 0.25 to 1.75
- param_bias: float32 [1024], P('replica'), may hold values from -3 to 3
- state_up: float32 [1024, 4096], P('replica', 'model'), may hold values from 0.0001953125 to 0.001953125
- state_down: float32 [4096, 1024], P('model', 'replica'), may hold values from 4.8828126e-05 to 0.00048828125
- state_query: float32 [1024, 1024], P('replica', 'model'), may hold values from 0.0001953125 to 0.001953125
- state_key: float32 [1024, 1024], P('replica', 'model'), may hold values from 0.0001953125 to 0.001953125
- state_value: float32 [1024, 1024], P('replica', 'model'), may hold values from 0.0001953125 to 0.001953125
- state_mixed: float32 [1024, 1024], P('model', 'replica'), may hold values from 0.0001953125 to 0.001953125
- state_norm: float32 [1024], P('replica'), may hold values from 0.05 to 0.8
- state_bias: float32 [1024], P('replica'), may hold values from 0.05 to 0.8
Outputs:
- half_up: bfloat16 [1024, 4096], P(None, 'model')
- half_down: bfloat16 [4096, 1024], P('model')
- half_query: bfloat16 [1024, 1024], P(None, 'model')
- half_key: bfloat16 [1024, 1024], P(None, 'model')
- half_value: bfloat16 [1024, 1024], P(None, 'model')
- half_mixed: bfloat16 [1024, 1024], P('model')
- half_norm: bfloat16 [1024], replicated
- half_bias: bfloat16 [1024], replicated
- next_up: float32 [1024, 4096], P('replica', 'model')
- next_down: float32 [4096, 1024], P('model', 'replica')
- next_query: float32 [1024, 1024], P('replica', 'model')
- next_key: float32 [1024, 1024], P('replica', 'model')
- next_value: float32 [1024, 1024], P('replica', 'model')
- next_mixed: float32 [1024, 1024], P('model', 'replica')
- next_norm: float32 [1024], P('replica')
- next_bias: float32 [1024], P('replica')
- state_new_up: float32 [1024, 4096], P('replica', 'model')
- state_new_down: float32 [4096, 1024], P('model', 'replica')
- state_new_query: float32 [1024, 1024], P('replica', 'model')
- state_new_key: float32 [1024, 1024], P('replica', 'model')
- state_new_value: float32 [1024, 1024], P('replica', 'model')
- state_new_mixed: float32 [1024, 1024], P('model', 'replica')
- state_new_norm: float32 [1024], P('replica')
- state_new_bias: float32 [1024], P('replica')
All inputs are finite; a program needn't handle non-finite values.
Results may differ from a plain program's by a relative error of at most 0.001.
Values may be sent and summed in bfloat16 or wider, within the bound.
A program may use at most 64 MiB of HBM per device.

v0:
```python
import jax
import jax.numpy as jnp
from jax import lax
from jax.sharding import PartitionSpec as P

learn_rate = 0.025
hold_rate = 0.7


def local(
    slope_up,
    slope_down,
    slope_query,
    slope_key,
    slope_value,
    slope_mixed,
    slope_norm,
    slope_bias,
    param_up,
    param_down,
    param_query,
    param_key,
    param_value,
    param_mixed,
    param_norm,
    param_bias,
    state_up,
    state_down,
    state_query,
    state_key,
    state_value,
    state_mixed,
    state_norm,
    state_bias,
):
    mean_up, mean_down, mean_query, mean_key, mean_value, mean_mixed = (
        lax.psum_scatter(slope_up[0], "replica", scatter_dimension=0, tiled=True),
        lax.psum_scatter(slope_down[0], "replica", scatter_dimension=1, tiled=True),
        lax.psum_scatter(slope_query[0], "replica", scatter_dimension=0, tiled=True),
        lax.psum_scatter(slope_key[0], "replica", scatter_dimension=0, tiled=True),
        lax.psum_scatter(slope_value[0], "replica", scatter_dimension=0, tiled=True),
        lax.psum_scatter(slope_mixed[0], "replica", scatter_dimension=1, tiled=True),
    )
    whole_norm, whole_bias = lax.psum((slope_norm[0], slope_bias[0]), "replica")
    place = lax.axis_index("replica")
    mean_norm = lax.dynamic_slice_in_dim(
        whole_norm, place * param_norm.shape[0], param_norm.shape[0]
    )
    mean_bias = lax.dynamic_slice_in_dim(
        whole_bias, place * param_bias.shape[0], param_bias.shape[0]
    )
    mean_rate = lax.axis_size("replica") ** (-0.5)
    mean_up = mean_up * mean_rate
    mean_down = mean_down * mean_rate
    mean_query = mean_query * mean_rate
    mean_key = mean_key * mean_rate
    mean_value = mean_value * mean_rate
    mean_mixed = mean_mixed * mean_rate
    mean_norm = mean_norm * mean_rate
    mean_bias = mean_bias * mean_rate
    (
        own_up,
        own_down,
        own_query,
        own_key,
        own_value,
        own_mixed,
        slope_up_norm,
        slope_down_norm,
        slope_query_norm,
        slope_key_norm,
        slope_value_norm,
        slope_mixed_norm,
    ) = lax.psum(
        (
            jnp.sum(param_up * param_up, axis=1, keepdims=True),
            jnp.sum(param_down * param_down, axis=0, keepdims=True),
            jnp.sum(param_query * param_query, axis=1, keepdims=True),
            jnp.sum(param_key * param_key, axis=1, keepdims=True),
            jnp.sum(param_value * param_value, axis=1, keepdims=True),
            jnp.sum(param_mixed * param_mixed, axis=0, keepdims=True),
            jnp.sum(mean_up * mean_up, axis=1, keepdims=True),
            jnp.sum(mean_down * mean_down, axis=0, keepdims=True),
            jnp.sum(mean_query * mean_query, axis=1, keepdims=True),
            jnp.sum(mean_key * mean_key, axis=1, keepdims=True),
            jnp.sum(mean_value * mean_value, axis=1, keepdims=True),
            jnp.sum(mean_mixed * mean_mixed, axis=0, keepdims=True),
        ),
        "model",
    )
    mean_up = mean_up * (jnp.sqrt(own_up) * lax.rsqrt(slope_up_norm + 1e-06))
    mean_down = mean_down * (jnp.sqrt(own_down) * lax.rsqrt(slope_down_norm + 1e-06))
    mean_query = mean_query * (jnp.sqrt(own_query) * lax.rsqrt(slope_query_norm + 1e-06))
    mean_key = mean_key * (jnp.sqrt(own_key) * lax.rsqrt(slope_key_norm + 1e-06))
    mean_value = mean_value * (jnp.sqrt(own_value) * lax.rsqrt(slope_value_norm + 1e-06))
    mean_mixed = mean_mixed * (jnp.sqrt(own_mixed) * lax.rsqrt(slope_mixed_norm + 1e-06))
    state_new_up = hold_rate * state_up + (1.0 - hold_rate) * mean_up * mean_up
    next_up = param_up - learn_rate * mean_up * lax.rsqrt(state_new_up + 1e-06)
    state_new_down = hold_rate * state_down + (1.0 - hold_rate) * mean_down * mean_down
    next_down = param_down - learn_rate * mean_down * lax.rsqrt(state_new_down + 1e-06)
    state_new_query = hold_rate * state_query + (1.0 - hold_rate) * mean_query * mean_query
    next_query = param_query - learn_rate * mean_query * lax.rsqrt(state_new_query + 1e-06)
    state_new_key = hold_rate * state_key + (1.0 - hold_rate) * mean_key * mean_key
    next_key = param_key - learn_rate * mean_key * lax.rsqrt(state_new_key + 1e-06)
    state_new_value = hold_rate * state_value + (1.0 - hold_rate) * mean_value * mean_value
    next_value = param_value - learn_rate * mean_value * lax.rsqrt(state_new_value + 1e-06)
    state_new_mixed = hold_rate * state_mixed + (1.0 - hold_rate) * mean_mixed * mean_mixed
    next_mixed = param_mixed - learn_rate * mean_mixed * lax.rsqrt(state_new_mixed + 1e-06)
    state_new_norm = hold_rate * state_norm + (1.0 - hold_rate) * mean_norm * mean_norm
    next_norm = param_norm - learn_rate * mean_norm * lax.rsqrt(state_new_norm + 1e-06)
    state_new_bias = hold_rate * state_bias + (1.0 - hold_rate) * mean_bias * mean_bias
    next_bias = param_bias - learn_rate * mean_bias * lax.rsqrt(state_new_bias + 1e-06)
    half_up, half_down, half_query, half_key, half_value, half_mixed, half_norm, half_bias = (
        lax.all_gather(next_up.astype(jnp.bfloat16), "replica", axis=0, tiled=True),
        lax.all_gather(next_down.astype(jnp.bfloat16), "replica", axis=1, tiled=True),
        lax.all_gather(next_query.astype(jnp.bfloat16), "replica", axis=0, tiled=True),
        lax.all_gather(next_key.astype(jnp.bfloat16), "replica", axis=0, tiled=True),
        lax.all_gather(next_value.astype(jnp.bfloat16), "replica", axis=0, tiled=True),
        lax.all_gather(next_mixed.astype(jnp.bfloat16), "replica", axis=1, tiled=True),
        lax.all_gather(next_norm.astype(jnp.bfloat16), "replica", axis=0, tiled=True),
        lax.all_gather(next_bias.astype(jnp.bfloat16), "replica", axis=0, tiled=True),
    )
    return (
        half_up,
        half_down,
        half_query,
        half_key,
        half_value,
        half_mixed,
        half_norm,
        half_bias,
        next_up,
        next_down,
        next_query,
        next_key,
        next_value,
        next_mixed,
        next_norm,
        next_bias,
        state_new_up,
        state_new_down,
        state_new_query,
        state_new_key,
        state_new_value,
        state_new_mixed,
        state_new_norm,
        state_new_bias,
    )


def solution(mesh):
    placed = (
        P("replica", None, "model"),
        P("replica", "model", None),
        P("replica", None, "model"),
        P("replica", None, "model"),
        P("replica", None, "model"),
        P("replica", "model", None),
        P("replica", None),
        P("replica", None),
        P("replica", "model"),
        P("model", "replica"),
        P("replica", "model"),
        P("replica", "model"),
        P("replica", "model"),
        P("model", "replica"),
        P("replica"),
        P("replica"),
        P("replica", "model"),
        P("model", "replica"),
        P("replica", "model"),
        P("replica", "model"),
        P("replica", "model"),
        P("model", "replica"),
        P("replica"),
        P("replica"),
    )
    return jax.shard_map(
        local,
        mesh=mesh,
        in_specs=placed,
        out_specs=(
            P(None, "model"),
            P("model", None),
            P(None, "model"),
            P(None, "model"),
            P(None, "model"),
            P("model", None),
            P(),
            P(),
            P("replica", "model"),
            P("model", "replica"),
            P("replica", "model"),
            P("replica", "model"),
            P("replica", "model"),
            P("model", "replica"),
            P("replica"),
            P("replica"),
            P("replica", "model"),
            P("model", "replica"),
            P("replica", "model"),
            P("replica", "model"),
            P("replica", "model"),
            P("model", "replica"),
            P("replica"),
            P("replica"),
        ),
        check_vma=False,
    )
```

profile of v0, /device:TPU:10, one launch (start us, length us, event | category | flops | bytes accessed | tf_op | source)
XLA Modules:
  0.0 668.9 jit_solution(12016515698589686928)
XLA Ops:
  12.2 64.7 %reduce-scatter.11.cloned.1.call-done = f32[128,256]{1,0:T(8,128)} async-done(((f32[1024,256]{1,0:T(8,128)}), f32[128,256]{1,0:T(8,128)}) %reduce-scatter.11.cloned.1.call-update) | async-done | bytes 131088 | tf_op jit(solution)/shard_map/reduce_scatter | solution.py:39
  77.0 1.0 multiply_reduce_fusion.10
  78.0 65.9 %reduce-scatter.13.cloned.1.call-done = f32[128,256]{1,0:T(8,128)} async-done(((f32[1024,256]{1,0:T(8,128)}), f32[128,256]{1,0:T(8,128)}) %reduce-scatter.13.cloned.1.call-update) | async-done | bytes 131088 | tf_op jit(solution)/shard_map/reduce_scatter | solution.py:40
  143.9 1.0 multiply_reduce_fusion.8
  144.9 65.9 %reduce-scatter.15.cloned.1.call-done = f32[128,256]{1,0:T(8,128)} async-done(((f32[1024,256]{1,0:T(8,128)}), f32[128,256]{1,0:T(8,128)}) %reduce-scatter.15.cloned.1.call-update) | async-done | bytes 131088 | tf_op jit(solution)/shard_map/reduce_scatter | solution.py:41
  210.8 1.0 multiply_reduce_fusion.6
  211.8 65.9 %reduce-scatter.17.cloned.1.call-done = f32[256,128]{1,0:T(8,128)} async-done(((f32[256,1024]{1,0:T(8,128)}), f32[256,128]{1,0:T(8,128)}) %reduce-scatter.17.cloned.1.call-update) | async-done | bytes 131088 | tf_op jit(solution)/shard_map/reduce_scatter | solution.py:42
  277.7 1.0 multiply_reduce_fusion.4
  278.7 90.3 %reduce-scatter.7.cloned.1.call-done = f32[128,1024]{1,0:T(8,128)} async-done(((f32[1024,1024]{1,0:T(8,128)}), f32[128,1024]{1,0:T(8,128)}) %reduce-scatter.7.cloned.1.call-update) | async-done | bytes 524304 | tf_op jit(solution)/shard_map/reduce_scatter | solution.py:37
  369.0 1.2 multiply_reduce_fusion.2
  370.3 90.2 %reduce-scatter.9.cloned.1.call-done = f32[1024,128]{1,0:T(8,128)} async-done(((f32[1024,1024]{1,0:T(8,128)}), f32[1024,128]{1,0:T(8,128)}) %reduce-scatter.9.cloned.1.call-update) | async-done | bytes 524304 | tf_op jit(solution)/shard_map/reduce_scatter | solution.py:38
  460.5 1.2 multiply_reduce_fusion
  461.7 6.1 all-reduce.1
  467.8 2.3 fusion.14
  470.3 1.3 fusion.16
  471.6 17.7 %all-reduce = (f32[1024]{0:T(1024)S(1)}, f32[1024]{0:T(1024)S(1)}) all-reduce(f32[1024]{0:T(1024)S(1)} %bitcast.44, f32[1024]{0:T(1024)S(1)} %bitcast.45), channel_id=1, replica_groups=mesh['replica'=8,'model'=4] {'replica'}, use_global_device_ids=true, to_apply=%region_30.0 | all-reduce | flops 2048 | bytes 16384 | tf_op jit(solution)/shard_map/psum | solution.py:44
  489.9 16.4 %all-gather = bf16[8,1,128]{2,1,0:T(2,128)(2,1)S(1)} all-gather(bf16[1,1,128]{2,1,0:T(2,128)(2,1)S(1)} %get-tuple-element.41), channel_id=1, replica_groups=mesh['replica'=8,'model'=4] {'replica'}, dimensions={0}, use_global_device_ids=true | all-gather | bytes 2304 | tf_op jit(solution)/shard_map/all_gather | solution.py:120
  507.5 18.7 %all-gather.1 = bf16[8,1,128]{2,1,0:T(2,128)(2,1)S(1)} all-gather(bf16[1,1,128]{2,1,0:T(2,128)(2,1)S(1)} %get-tuple-element.38), channel_id=1, replica_groups=mesh['replica'=8,'model'=4] {'replica'}, dimensions={0}, use_global_device_ids=true | all-gather | bytes 2304 | tf_op jit(solution)/shard_map/all_gather | solution.py:121
  526.8 0.8 fusion.10
  527.6 33.4 %all_gather.27 = bf16[1024,256]{1,0:T(8,128)(2,1)S(1)} all-gather(bf16[128,256]{1,0:T(8,128)(2,1)S(1)} %get-tuple-element.50), channel_id=1, replica_groups=mesh['replica'=8,'model'=4] {'replica'}, dimensions={0}, use_global_device_ids=true | all-gather | bytes 589824 | tf_op jit(solution)/shard_map/all_gather | solution.py:117
  561.0 0.8 fusion.8
  561.8 32.1 %all_gather.28 = bf16[1024,256]{1,0:T(8,128)(2,1)S(1)} all-gather(bf16[128,256]{1,0:T(8,128)(2,1)S(1)} %get-tuple-element.47), channel_id=1, replica_groups=mesh['replica'=8,'model'=4] {'replica'}, dimensions={0}, use_global_device_ids=true | all-gather | bytes 589824 | tf_op jit(solution)/shard_map/all_gather | solution.py:118
  593.9 0.7 fusion.6
  594.6 29.2 %all_gather.29 = bf16[256,1024]{1,0:T(8,128)(2,1)S(1)} all-gather(bf16[256,128]{1,0:T(8,128)(2,1)S(1)} %get-tuple-element.44), channel_id=1, replica_groups=mesh['replica'=8,'model'=4] {'replica'}, dimensions={1}, use_global_device_ids=true | all-gather | bytes 589824 | tf_op jit(solution)/shard_map/all_gather | solution.py:119
  623.9 0.8 fusion.12
  624.7 29.6 %all_gather.26 = bf16[1024,256]{1,0:T(8,128)(2,1)S(1)} all-gather(bf16[128,256]{1,0:T(8,128)(2,1)S(1)} %get-tuple-element.53), channel_id=1, replica_groups=mesh['replica'=8,'model'=4] {'replica'}, dimensions={0}, use_global_device_ids=true | all-gather | bytes 589824 | tf_op jit(solution)/shard_map/all_gather | solution.py:116
  654.3 3.2 copy.54
  657.5 1.3 copy.55
  658.8 0.8 copy.56
  659.6 0.8 copy.57
  660.4 0.8 copy.58
  661.2 0.8 copy.59
  (79 shorter events, 7.4 us)
Async XLA Ops:
  7.2 69.8 %reduce-scatter.11.cloned.1.call-start = ((), (), s32[]{:S(2)}) async-start(), calls=%async_computation.10 | async-start | bytes 1179648 | tf_op jit(solution)/shard_map/reduce_scatter | solution.py:39
  7.9 136.0 %reduce-scatter.13.cloned.1.call-start = ((), (), s32[]{:S(2)}) async-start(), calls=%async_computation.11 | async-start | bytes 1179648 | tf_op jit(solution)/shard_map/reduce_scatter | solution.py:40
  8.7 202.2 %reduce-scatter.15.cloned.1.call-start = ((), (), s32[]{:S(2)}) async-start(), calls=%async_computation.12 | async-start | bytes 1179648 | tf_op jit(solution)/shard_map/reduce_scatter | solution.py:41
  9.4 268.3 %reduce-scatter.17.cloned.1.call-start = ((), (), s32[]{:S(2)}) async-start(), calls=%async_computation.13 | async-start | bytes 1179648 | tf_op jit(solution)/shard_map/reduce_scatter | solution.py:42
  10.0 359.0 %reduce-scatter.7.cloned.1.call-start = ((), (), s32[]{:S(2)}) async-start(), calls=%async_computation.6 | async-start | bytes 4718592 | tf_op jit(solution)/shard_map/reduce_scatter | solution.py:37
  10.6 449.9 %reduce-scatter.9.cloned.1.call-start = ((), (), s32[]{:S(2)}) async-start(), calls=%async_computation.8 | async-start | bytes 4718592 | tf_op jit(solution)/shard_map/reduce_scatter | solution.py:38
  10.6 0.9 copy-start.4
  10.6 1.0 copy-start.5
  10.6 1.1 copy-start.6
  10.7 1.2 copy-start.7
  10.7 1.3 copy-start.2
  10.7 1.4 copy-start.1
  11.2 456.6 %copy-start.12 = (f32[1024,128]{1,0:T(8,128)S(1)}, f32[1024,128]{1,0:T(8,128)}, u32[]{:S(2)}) copy-start(f32[1024,128]{1,0:T(8,128)} %param.41) | copy-start | bytes 1572868
  11.2 643.1 %all-gather.7.cloned.1.call-start = ((), (), s32[]{:S(2)}) async-start(), calls=%async_computation.9 | async-start | bytes 2359296 | tf_op jit(solution)/shard_map/all_gather | solution.py:115
  278.7 191.5 %copy-start.13 = (f32[128,1024]{1,0:T(8,128)S(1)}, f32[128,1024]{1,0:T(8,128)}, u32[]{:S(2)}) copy-start(f32[128,1024]{1,0:T(8,128)} %param.40) | copy-start | bytes 1572868
  369.0 101.2 %copy-start.3 = (f32[128,1024]{1,0:T(8,128)S(1)}, f32[128,1024]{1,0:T(8,128)}, u32[]{:S(2)}) copy-start(f32[128,1024]{1,0:T(8,128)} %reduce-scatter.7.cloned.1.call-done) | copy-start | bytes 1572868
  470.1 1.5 copy-start.18
  470.1 1.5 copy-start.19
  470.1 19.2 %copy-start.20 = (f32[128]{0:T(128)S(1)}, f32[128]{0:T(128)}, u32[]{:S(2)}) copy-start(f32[128]{0:T(128)} %param.38) | copy-start | bytes 1540
  470.1 19.2 %copy-start.21 = (f32[128]{0:T(128)S(1)}, f32[128]{0:T(128)}, u32[]{:S(2)}) copy-start(f32[128]{0:T(128)} %param.46) | copy-start | bytes 1540
  470.1 36.9 %copy-start.22 = (f32[128]{0:T(128)S(1)}, f32[128]{0:T(128)}, u32[]{:S(2)}) copy-start(f32[128]{0:T(128)} %param.39) | copy-start | bytes 1540
  470.1 36.8 %copy-start.23 = (f32[128]{0:T(128)S(1)}, f32[128]{0:T(128)}, u32[]{:S(2)}) copy-start(f32[128]{0:T(128)} %param.47) | copy-start | bytes 1540
  470.1 56.7 %copy-start.9 = (f32[128,256]{1,0:T(8,128)S(1)}, f32[128,256]{1,0:T(8,128)}, u32[]{:S(2)}) copy-start(f32[128,256]{1,0:T(8,128)} %reduce-scatter.13.cloned.1.call-done) | copy-start | bytes 393220
  470.1 56.7 %copy-start.14 = (f32[128,256]{1,0:T(8,128)S(1)}, f32[128,256]{1,0:T(8,128)}, u32[]{:S(2)}) copy-start(f32[128,256]{1,0:T(8,128)} %param.43) | copy-start | bytes 393220
  470.1 184.1 %all-gather.5.cloned.1.call-start = ((), (), s32[]{:S(2)}) async-start(), calls=%async_computation.7 | async-start | bytes 2359296 | tf_op jit(solution)/shard_map/all_gather | solution.py:114
  470.2 90.8 %copy-start.10 = (f32[128,256]{1,0:T(8,128)S(1)}, f32[128,256]{1,0:T(8,128)}, u32[]{:S(2)}) copy-start(f32[128,256]{1,0:T(8,128)} %reduce-scatter.15.cloned.1.call-done) | copy-start | bytes 393220
  470.2 90.8 %copy-start.15 = (f32[128,256]{1,0:T(8,128)S(1)}, f32[128,256]{1,0:T(8,128)}, u32[]{:S(2)}) copy-start(f32[128,256]{1,0:T(8,128)} %param.44) | copy-start | bytes 393220
  471.5 122.3 %copy-start.11 = (f32[256,128]{1,0:T(8,128)S(1)}, f32[256,128]{1,0:T(8,128)}, u32[]{:S(2)}) copy-start(f32[256,128]{1,0:T(8,128)} %reduce-scatter.17.cloned.1.call-done) | copy-start | bytes 393220
  471.5 122.3 %copy-start.16 = (f32[256,128]{1,0:T(8,128)S(1)}, f32[256,128]{1,0:T(8,128)}, u32[]{:S(2)}) copy-start(f32[256,128]{1,0:T(8,128)} %param.45) | copy-start | bytes 393220
  471.6 152.3 %copy-start.8 = (f32[128,256]{1,0:T(8,128)S(1)}, f32[128,256]{1,0:T(8,128)}, u32[]{:S(2)}) copy-start(f32[128,256]{1,0:T(8,128)} %reduce-scatter.11.cloned.1.call-done) | copy-start | bytes 393220
  471.6 152.3 %copy-start.17 = (f32[128,256]{1,0:T(8,128)S(1)}, f32[128,256]{1,0:T(8,128)}, u32[]{:S(2)}) copy-start(f32[128,256]{1,0:T(8,128)} %param.42) | copy-start | bytes 393220
  654.3 3.2 copy-start
Sparse Core Ops, SparseCore 0:
  11.4 65.5 reduce-scatter.10
  80.4 63.4 reduce-scatter.12
  147.3 63.4 reduce-scatter.14
  214.1 63.5 reduce-scatter.16
  281.2 87.7 reduce-scatter.6
  372.5 87.9 reduce-scatter.8
  470.3 48.1 all-gather.6
  521.2 56.0 all-gather.4
where the time goes:
time: 674 us; the launch traced here: 669 us
  waiting for transfers between devices  447 us (66%)
  blocking collectives  183 us (27%)
  other arithmetic  16.2 us (2%)
  between operations  14.5 us (2%)
  local copies, waits for them, and re-layouts  8.19 us (1%)
    reduce_scatter x1, waiting for transfers between devices, local(): lax.psum_scatter(slope_up[0], 'replica', scatter_dimension=0, tiled=True)  90.3 us
    reduce_scatter x1, waiting for transfers between devices, local(): lax.psum_scatter(slope_down[0], 'replica', scatter_dimension=1, tiled=True)  90.2 us
    reduce_scatter x1, waiting for transfers between devices, local(): lax.psum_scatter(slope_value[0], 'replica', scatter_dimension=0, tiled=True)  65.9 us
    reduce_scatter x1, waiting for transfers between devices, local(): lax.psum_scatter(slope_key[0], 'replica', scatter_dimension=0, tiled=True)  65.9 us
    reduce_scatter x1, waiting for transfers between devices, local(): lax.psum_scatter(slope_mixed[0], 'replica', scatter_dimension=1, tiled=True)  65.9 us
    reduce_scatter x1, waiting for transfers between devices, local(): lax.psum_scatter(slope_query[0], 'replica', scatter_dimension=0, tiled=True)  64.7 us
    all_gather x1, blocking collectives, local(): lax.all_gather(next_key.astype(jnp.bfloat16), 'replica', axis=0, tiled=True)  33.4 us
    all_gather x1, blocking collectives, local(): lax.all_gather(next_value.astype(jnp.bfloat16), 'replica', axis=0, tiled=...  32.1 us
  transfers between devices with their start and end apart: 8, of which 6 were waited for; matrix products, arithmetic and copies ran while one was open for 2% of the time, Pallas kernels for 0%

commit v1 on v0

--- a/solution.py
+++ b/solution.py
@@ -1,13 +1,522 @@
+import functools
+
 import jax
 import jax.numpy as jnp
 from jax import lax
+from jax.experimental import pallas as pl
+from jax.experimental.pallas import tpu as pltpu
 from jax.sharding import PartitionSpec as P
 
 learn_rate = 0.025
 hold_rate = 0.7
-
-
-def local(
+root = 9
+MESH = pl.DeviceIdType.MESH
+
+
+class Group:
+    def __init__(self, members, rows, near_first):
+        self.members = members
+        self.rows = rows
+        self.near_first = near_first
+
+
+UP, DOWN, MIXED, QKV = range(4)
+GROUPS = (
+    Group((0,), True, False),
+    Group((1,), False, False),
+    Group((5,), False, False),
+    Group((2, 3, 4), True, True),
+)
+ORDER = ((1, 1), (0, 1), (1, 0), (0, 0))
+
+
+def kernel(replicas, models, limit, shapes, *refs):
+    slopes, slope_norm, slope_bias = refs[0:6], refs[6], refs[7]
+    params, param_norm, param_bias = refs[8:14], refs[14], refs[15]
+    states, state_norm, state_bias = refs[16:22], refs[22], refs[23]
+    halves, half_norm, half_bias = refs[24:30], refs[30], refs[31]
+    nexts, next_norm, next_bias = refs[32:38], refs[38], refs[39]
+    news, new_norm, new_bias = refs[40:46], refs[46], refs[47]
+    scratch = list(refs[48:])
+    groups = range(len(GROUPS))
+    take = lambda: [scratch.pop(0) for _ in groups]
+    xin, enc1, rec1, enc2, rec2, enc3, rec3, own, st, full, sq, sqr = (take() for _ in range(12))
+    vs, vown, vrec, vnext, vag = (scratch.pop(0) for _ in range(5))
+    rs_s, rs_r, ag_s, ag_r, n_s, n_r, v_s, v_r, w_s, w_r = (scratch.pop(0) for _ in range(10))
+    load_sem, own_sem, st_sem, half_sem, next_sem, new_sem, vown_sem = scratch
+
+    r = lax.axis_index("replica")
+    m = lax.axis_index("model")
+    far, near, y = r // 4, (r // 2) % 2, r % 2
+    bit = lambda v, k: v if k == 0 else 1 - v
+    place = lambda k2, k1, ky: (bit(far, k2) * 2 + bit(near, k1)) * 2 + bit(y, ky)
+    y_peer, near_peer, far_peer = place(0, 0, 1), place(0, 1, 0), place(1, 0, 0)
+
+    scale = 2.0**13 / (limit * replicas)
+    rate = replicas ** (-0.5)
+
+    def encode(x):
+        t = x * scale
+        t2 = t * t
+        t4 = t2 * t2
+        return (t4 * t4 * t).astype(jnp.bfloat16)
+
+    def decode(c):
+        f = c.astype(jnp.float32)
+        a = jnp.exp(jnp.log(jnp.abs(f)) * (1.0 / root)) * (1.0 / scale)
+        return jnp.where(f < 0, -a, a)
+
+    def block(g, kf, ks, kt):
+        return kt * 4 + (kf * 2 + ks if GROUPS[g].near_first else ks * 2 + kf)
+
+    def slab(g, b, ref, i):
+        at = place(b // 4, (b // 2) % 2, b % 2)
+        h, w = shapes[g]
+        if GROUPS[g].rows:
+            return ref.at[pl.ds(pl.multiple_of(at * h, h), h), :]
+        return ref.at[:, pl.ds(pl.multiple_of(at * w, w), w)]
+
+    def lanes(g, ref, i):
+        n = len(GROUPS[g].members)
+        w = shapes[g][1] // n
+        return ref if n == 1 else ref.at[:, i * w : (i + 1) * w]
+
+    def loop(g, body):
+        h, w = shapes[g]
+        step = min(h, max(16, 16 * 1024 // w // 16 * 16))
+        while h % step:
+            step -= 16
+        lax.fori_loop(0, h // step, lambda i, c: (body(pl.ds(pl.multiple_of(i * step, step), step)), c)[1], 0)
+
+    def remote(src, dst, s, d, peer, axis="replica"):
+        return pltpu.make_async_remote_copy(
+            src_ref=src, dst_ref=dst, send_sem=s, recv_sem=d, device_id={axis: peer}, device_id_type=MESH
+        )
+
+    barrier = pltpu.get_barrier_semaphore()
+    for j in range(1, replicas):
+        pl.semaphore_signal(barrier, inc=1, device_id={"replica": lax.rem(r + j, replicas)}, device_id_type=MESH)
+    for j in range(1, models):
+        pl.semaphore_signal(barrier, inc=1, device_id={"model": lax.rem(m + j, models)}, device_id_type=MESH)
+
+    def load(g, b):
+        for i, a in enumerate(GROUPS[g].members):
+            pltpu.make_async_copy(
+                slab(g, b, slopes[a].at[0], i), lanes(g, xin[g].at[b], i), load_sem.at[g, b]
+            ).start()
+
+    def loaded(g, b):
+        pltpu.make_async_copy(xin[g].at[b], xin[g].at[b], load_sem.at[g, b]).wait()
+
+    for kt, ks in ORDER:
+        load(UP, block(UP, 1, ks, kt))
+        load(QKV, block(QKV, 1, ks, kt))
+    for kt, ks in ORDER:
+        load(QKV, block(QKV, 0, ks, kt))
+    for g in (DOWN, MIXED):
+        for kt, ks in ORDER:
+            load(g, block(g, 1, ks, kt))
+    for g in groups:
+        for i, a in enumerate(GROUPS[g].members):
+            pltpu.make_async_copy(params[a], lanes(g, own[g], i), own_sem.at[g]).start()
+            pltpu.make_async_copy(states[a], lanes(g, st[g], i), st_sem.at[g]).start()
+    for g in (UP, DOWN, MIXED):
+        for kt, ks in ORDER:
+            load(g, block(g, 0, ks, kt))
+
+    def peer_of(g, stage):
+        if stage == 3:
+            return far_peer
+        return near_peer if (stage == 1) == GROUPS[g].near_first else y_peer
+
+    def copy1(g, i):
+        return remote(enc1[g].at[i], rec1[g].at[i], rs_s.at[g, i], rs_r.at[g, i], peer_of(g, 1))
+
+    def copy2(g, kt):
+        return remote(enc2[g].at[kt], rec2[g].at[kt], rs_s.at[g, 4 + kt], rs_r.at[g, 4 + kt], peer_of(g, 2))
+
+    def copy3(g):
+        return remote(enc3[g], rec3[g], rs_s.at[g, 6], rs_r.at[g, 6], peer_of(g, 3))
+
+    def encode1(g, i):
+        kt, ks = ORDER[i]
+        b = block(g, 1, ks, kt)
+        loaded(g, b)
+        src, dst = xin[g].at[b], enc1[g].at[i]
+
+        def body(d):
+            dst[d, :] = encode(src[d, :])
+
+        loop(g, body)
+
+    def add(g, b, rec):
+        acc = xin[g].at[b]
+
+        def body(d):
+            acc[d, :] = acc[d, :] + decode(rec[d, :])
+
+        loop(g, body)
+
+    def add_encode(g, b, rec, dst):
+        acc = xin[g].at[b]
+
+        def body(d):
+            dst[d, :] = encode(acc[d, :] + decode(rec[d, :]))
+
+        loop(g, body)
+
+    def take1(g, i):
+        kt, ks = ORDER[i]
+        b = block(g, 0, ks, kt)
+        loaded(g, b)
+        copy1(g, i).wait_recv()
+        if ks:
+            add_encode(g, b, rec1[g].at[i], enc2[g].at[kt])
+            copy2(g, kt).start()
+        else:
+            add(g, b, rec1[g].at[i])
+
+    def take2(g, kt):
+        b = block(g, 0, 0, kt)
+        copy2(g, kt).wait_recv()
+        if kt:
+            add_encode(g, b, rec2[g].at[kt], enc3[g])
+            copy3(g).start()
+        else:
+            add(g, b, rec2[g].at[kt])
+
+    def fold(x):
+        w = x.shape[1]
+        total = x[:, 0:128]
+        for k in range(128, w, 128):
+            total = total + x[:, k : k + 128]
+        return total
+
+    def squares(g, which, read):
+        h, w = shapes[g]
+        if GROUPS[g].rows:
+            n = len(GROUPS[g].members)
+
+            def body(d):
+                v = read(d)
+                v = v * v
+                for i in range(n):
+                    sq[g][which, i, d, :] = fold(v[:, i * (w // n) : (i + 1) * (w // n)])
+
+            loop(g, body)
+        else:
+            sq[g][which] = jnp.zeros((8, w), jnp.float32)
+
+            def body(d):
+                v = read(d)
+                sq[g][which] += jnp.sum((v * v).reshape(-1, 8, w), axis=0)
+
+            loop(g, body)
+
+    def copyn(g, j):
+        return remote(
+            sq[g], sqr[g].at[j - 1], n_s.at[g, j - 1], n_r.at[g, j - 1], lax.rem(m + j, models), "model"
+        )
+
+    def own_squares(g):
+        pltpu.make_async_copy(own[g], own[g], own_sem.at[g]).wait()
+        squares(g, 0, lambda d: own[g][d, :])
+
+    def take3(g):
+        copy3(g).wait_recv()
+        acc, rec = xin[g].at[0], rec3[g]
+
+        def read(d):
+            v = (acc[d, :] + decode(rec[d, :])) * rate
+            acc[d, :] = v
+            return v
+
+        squares(g, 1, read)
+        for j in range(1, models):
+            copyn(g, j).start()
+
+    def rule(p, s, v):
+        s = hold_rate * s + (1.0 - hold_rate) * v * v
+        return p - learn_rate * v * lax.rsqrt(s + 1e-06), s
+
+    def update(g):
+        h, w = shapes[g]
+        for j in range(1, models):
+            copyn(g, j).wait_recv()
+        pltpu.make_async_copy(st[g], st[g], st_sem.at[g]).wait()
+        acc, half = xin[g].at[0], full[g].at[0]
+
+        def ratio(index, axis):
+            p, s = sq[g][(0, *index)], sq[g][(1, *index)]
+            for j in range(models - 1):
+                p = p + sqr[g][(j, 0, *index)]
+                s = s + sqr[g][(j, 1, *index)]
+            p = jnp.sum(p, axis=axis, keepdims=True)
+            s = jnp.sum(s, axis=axis, keepdims=True)
+            return jnp.sqrt(p) * lax.rsqrt(s + 1e-06)
+
+        if GROUPS[g].rows:
+            n = len(GROUPS[g].members)
+
+            def body(d):
+                for i in range(n):
+                    cols = slice(i * (w // n), (i + 1) * (w // n))
+                    v = acc[d, cols] * ratio((i, d), 1)
+                    p, s = rule(own[g][d, cols], st[g][d, cols], v)
+                    own[g][d, cols] = p
+                    st[g][d, cols] = s
+                    half[d, cols] = p.astype(jnp.bfloat16)
+
+            loop(g, body)
+        else:
+            t = ratio((), 0)
+
+            def body(d):
+                p, s = rule(own[g][d, :], st[g][d, :], acc[d, :] * t)
+                own[g][d, :] = p
+                st[g][d, :] = s
+                half[d, :] = p.astype(jnp.bfloat16)
+
+            loop(g, body)
+        gather3(g).start()
+        put(g, 0)
+        for i, a in enumerate(GROUPS[g].members):
+            pltpu.make_async_copy(lanes(g, own[g], i), nexts[a], next_sem.at[g]).start()
+            pltpu.make_async_copy(lanes(g, st[g], i), news[a], new_sem.at[g]).start()
+
+    def put(g, b):
+        for i, a in enumerate(GROUPS[g].members):
+            pltpu.make_async_copy(lanes(g, full[g].at[b], i), slab(g, b, halves[a], i), half_sem.at[g]).start()
+
+    def gather3(g):
+        return remote(
+            full[g].at[0], full[g].at[block(g, 0, 0, 1)], ag_s.at[g, 6], ag_r.at[g, 6], peer_of(g, 3)
+        )
+
+    def gather2(g, kt):
+        return remote(
+            full[g].at[block(g, 0, 0, kt)],
+            full[g].at[block(g, 0, 1, kt)],
+            ag_s.at[g, 4 + kt],
+            ag_r.at[g, 4 + kt],
+            peer_of(g, 2),
+        )
+
+    def gather1(g, kt, ks):
+        i = kt * 2 + ks
+        return remote(
+            full[g].at[block(g, 0, ks, kt)],
+            full[g].at[block(g, 1, ks, kt)],
+            ag_s.at[g, i],
+            ag_r.at[g, i],
+            peer_of(g, 1),
+        )
+
+    def spread_own(g):
+        gather2(g, 0).start()
+        gather1(g, 0, 0).start()
+
+    def got3(g):
+        gather3(g).wait_recv()
+        gather2(g, 1).start()
+        gather1(g, 1, 0).start()
+        put(g, block(g, 0, 0, 1))
+
+    def got2(g, kt):
+        gather2(g, kt).wait_recv()
+        gather1(g, kt, 1).start()
+        put(g, block(g, 0, 1, kt))
+
+    def got1(g):
+        for kt, ks in ((0, 0), (1, 0), (0, 1), (1, 1)):
+            gather1(g, kt, ks).wait_recv()
+            put(g, block(g, 1, ks, kt))
+
+    width = vs.shape[1] // replicas
+
+    def vec_out(j):
+        to = lax.rem(r + j, replicas)
+        return remote(
+            vs.at[:, pl.ds(pl.multiple_of(to * width, width), width)],
+            vrec.at[j - 1], v_s.at[j - 1], v_r.at[j - 1], to,
+        )
+
+    def vec_back(j):
+        return remote(vnext, vag.at[j - 1], w_s.at[j - 1], w_r.at[j - 1], lax.rem(r + j, replicas))
+
+    def vec_update():
+        pltpu.make_async_copy(vown, vown, vown_sem).wait()
+        total = vown[...]
+        for j in range(1, replicas):
+            vec_out(j).wait_recv()
+            total = total + vrec[j - 1]
+        v = total * rate
+        p, s = rule(param_norm[...], state_norm[...], v[0:1, :])
+        next_norm[...] = p
+        new_norm[...] = s
+        vnext[0:1, :] = p
+        p, s = rule(param_bias[...], state_bias[...], v[1:2, :])
+        next_bias[...] = p
+        new_bias[...] = s
+        vnext[1:2, :] = p
+        for j in range(1, replicas):
+            vec_back(j).start()
+
+    def vec_finish():
+        half_norm[r] = vnext[0:1, :].astype(jnp.bfloat16)
+        half_bias[r] = vnext[1:2, :].astype(jnp.bfloat16)
+        for j in range(1, replicas):
+            vec_back(j).wait_recv()
+            at = lax.rem(r + replicas - j, replicas)
+            half_norm[at] = vag[j - 1, 0:1, :].astype(jnp.bfloat16)
+            half_bias[at] = vag[j - 1, 1:2, :].astype(jnp.bfloat16)
+
+    vs[0:1, :] = slope_norm[...]
+    vs[1:2, :] = slope_bias[...]
+    encode1(UP, 0)
+    encode1(QKV, 0)
+    pl.semaphore_wait(barrier, replicas + models - 2)
+    copy1(UP, 0).start()
+    copy1(QKV, 0).start()
+    for i in (1, 2, 3):
+        encode1(UP, i)
+        copy1(UP, i).start()
+        encode1(QKV, i)
+        copy1(QKV, i).start()
+    pltpu.make_async_copy(vs.at[:, pl.ds(pl.multiple_of(r * width, width), width)], vown, vown_sem).start()
+    for j in range(1, replicas):
+        vec_out(j).start()
+    for i in range(4):
+        encode1(DOWN, i)
+    for i in range(4):
+        encode1(MIXED, i)
+    for g in groups:
+        own_squares(g)
+    vec_update()
+    take1(QKV, 0)
+    take1(QKV, 1)
+    for g in (DOWN, MIXED):
+        for i in range(4):
+            copy1(g, i).start()
+    take1(QKV, 2)
+    take1(QKV, 3)
+    for i in range(4):
+        take1(UP, i)
+    take2(QKV, 1)
+    take2(UP, 1)
+    take2(QKV, 0)
+    take2(UP, 0)
+    take3(QKV)
+    take1(DOWN, 0)
+    take3(UP)
+    update(QKV)
+    spread_own(QKV)
+    take1(DOWN, 1)
+    update(UP)
+    spread_own(UP)
+    got3(QKV)
+    take1(DOWN, 2)
+    take1(DOWN, 3)
+    take2(DOWN, 1)
+    got3(UP)
+    got2(QKV, 0)
+    for i in range(4):
+        take1(MIXED, i)
+    take2(DOWN, 0)
+    take2(MIXED, 1)
+    take2(MIXED, 0)
+    got2(QKV, 1)
+    take3(DOWN)
+    take3(MIXED)
+    update(DOWN)
+    spread_own(DOWN)
+    update(MIXED)
+    spread_own(MIXED)
+    got2(UP, 0)
+    got2(UP, 1)
+    got3(DOWN)
+    got3(MIXED)
+    got2(DOWN, 0)
+    got2(MIXED, 0)
+    got2(DOWN, 1)
+    got2(MIXED, 1)
+    vec_finish()
+    for g in (QKV, UP, DOWN, MIXED):
+        got1(g)
+
+    for g in groups:
+        for i in range(4):
+            copy1(g, i).wait_send()
+        for kt in (0, 1):
+            copy2(g, kt).wait_send()
+            gather2(g, kt).wait_send()
+            for ks in (0, 1):
+                gather1(g, kt, ks).wait_send()
+        copy3(g).wait_send()
+        gather3(g).wait_send()
+        for j in range(1, models):
+            copyn(g, j).wait_send()
+        pltpu.make_async_copy(full[g], full[g], half_sem.at[g]).wait()
+        pltpu.make_async_copy(own[g], own[g], next_sem.at[g]).wait()
+        pltpu.make_async_copy(st[g], st[g], new_sem.at[g]).wait()
+    for j in range(1, replicas):
+        vec_out(j).wait_send()
+        vec_back(j).wait_send()
+
+
+def fused(replicas, models, *args):
+    slopes, params = args[0:6], args[8:14]
+    f32, bf16 = jnp.float32, jnp.bfloat16
+    vec = args[6].shape[1]
+    width = vec // replicas
+    row = lambda a: a.reshape(1, -1)
+    args = (*args[0:14], row(args[14]), row(args[15]), *args[16:22], row(args[22]), row(args[23]))
+    shapes = []
+    for g in GROUPS:
+        h, w = params[g.members[0]].shape
+        shapes.append((h, w * len(g.members)))
+    S = jax.ShapeDtypeStruct
+    outs = [S(a.shape[1:], bf16) for a in slopes] + [S((replicas, 1, width), bf16)] * 2
+    for _ in range(2):
+        outs += [S(a.shape, f32) for a in params] + [S((1, width), f32)] * 2
+    ANY, VM = pl.BlockSpec(memory_space=pl.ANY), pl.BlockSpec(memory_space=pltpu.VMEM)
+    part = [ANY] * 6 + [VM] * 2
+    scratch = []
+    for count, dtype in ((8, f32), (4, bf16), (4, bf16), (2, bf16), (2, bf16), (0, bf16), (0, bf16), (0, f32), (0, f32), (8, bf16)):
+        scratch += [pltpu.VMEM((count, *s) if count else s, dtype) for s in shapes]
+    sq = [(2, len(g.members), s[0], 128) if g.rows else (2, 8, s[1]) for g, s in zip(GROUPS, shapes)]
+    scratch += [pltpu.VMEM(s, f32) for s in sq]
+    scratch += [pltpu.VMEM((models - 1, *s), f32) for s in sq]
+    scratch += [
+        pltpu.VMEM((2, vec), f32),
+        pltpu.VMEM((2, width), f32),
+        pltpu.VMEM((replicas - 1, 2, width), f32),
+        pltpu.VMEM((2, width), f32),
+        pltpu.VMEM((replicas - 1, 2, width), f32),
+    ]
+    dma = pltpu.SemaphoreType.DMA
+    n = len(GROUPS)
+    scratch += [dma((n, 7))] * 4 + [dma((n, models - 1))] * 2 + [dma((replicas - 1,))] * 4
+    scratch += [dma((n, 8))] + [dma((n,))] * 5 + [dma(())]
+    out = pl.pallas_call(
+        functools.partial(kernel, replicas, models, 4.0, shapes),
+        out_shape=outs,
+        in_specs=part * 3,
+        out_specs=part * 3,
+        scratch_shapes=scratch,
+        compiler_params=pltpu.CompilerParams(
+            collective_id=0, has_side_effects=True, vmem_limit_bytes=60 * 1024 * 1024
+        ),
+    )(*args)
+    flat = lambda a: a.reshape(-1)
+    return (
+        *out[0:6], flat(out[6]), flat(out[7]),
+        *out[8:14], flat(out[14]), flat(out[15]),
+        *out[16:22], flat(out[22]), flat(out[23]),
+    )
+
+
+def plain(
     slope_up,
     slope_down,
     slope_query,
@@ -149,6 +658,14 @@
 
 
 def solution(mesh):
+    replicas, models = mesh.shape["replica"], mesh.shape["model"]
+
+    def local(*args):
+        ok = replicas == 2**3 and all(a.shape[k] % 128 == 0 for a in args[8:14] for k in (0, 1))
+        if ok and args[14].shape[0] % 128 == 0:
+            return fused(replicas, models, *args)
+        return plain(*args)
+
     placed = (
         P("replica", None, "model"),
         P("replica", "model", None),

time: 674 us -> 186 us (0.28)
  waiting for transfers between devices: 447 us -> 0 us
  blocking collectives: 183 us -> 0 us
  Pallas kernels: 0 us -> 164 us
  between operations: 14.5 us -> 0.73 us
  other arithmetic: 16.2 us -> 2.56 us
  local copies, waits for them, and re-layouts: 8.19 us -> 18.3 us
    reduce_scatter x6 -> x0, waiting for transfers between devices: 443 us -> none  [the longest x1 90.3 us: local(): lax.psum_scatter(slope_up[0], 'replica', scatter_dimension=0, tiled=True)]
    pallas_call x0 -> x1, Pallas kernels: none -> 164 us  [fused(): pl.pallas_call(functools.partial(kernel, replicas, models, 4.0, shapes),...]
    all_gather x6 -> x0, blocking collectives: 159 us -> none  [the longest x1 33.4 us: local(): lax.all_gather(next_key.astype(jnp.bfloat16), 'replica', axis=0, tiled=True)]
    psum x2 -> x0, blocking collectives: 23.7 us -> none  [the longest x1 17.7 us: local(): whole_norm, whole_bias = lax.psum((slope_norm[0], slope_bias[0]), 'replica')]
    unnamed x54 -> x64, local copies, waits for them, and re-layouts: 8.19 us -> 18.3 us
    reduce_sum x12 -> x0, other arithmetic: 7.04 us -> none  [the longest x1 1.25 us: local(): jnp.sum(mean_up * mean_up, axis=1, keepdims=True)]
  transfers between devices with their start and end apart: 8 -> 0, of which waited for: 6 -> 0; matrix products, arithmetic and copies ran while one was open for 2% -> 0% of each run, Pallas kernels for 0% -> 0%
where the time goes in v1:
time: 186 us
  Pallas kernels  164 us (88%)
  local copies, waits for them, and re-layouts  18.3 us (10%)
  other arithmetic  2.56 us (1%)
    pallas_call x1, Pallas kernels, fused(): pl.pallas_call(functools.partial(kernel, replicas, models, 4.0, shapes),...  164 us
    unnamed x64, local copies, waits for them, and re-layouts  18.3 us

profile of v1, /device:TPU:10, one launch (start us, length us, event | category | flops | bytes accessed | tf_op | source)
XLA Modules:
  0.0 185.5 jit_solution(18258616809647597856)
XLA Ops:
  0.7 163.9 %shard_map.415 = (bf16[1024,1024]{1,0:T(8,128)(2,1)}, bf16[1024,1024]{1,0:T(8,128)(2,1)}, bf16[1024,256]{1,0:T(8,128)(2,1)}, bf16[1024,256]{1,0:T(8,128)(2,1)}, ...) custom-call(f32[1,1024,1024]{2,1,0:T(8,128)} %refs_0_.1, ...), custom_call_target="tpu_custom_call" | custom-call | tf_op jit(solution)/shard_map/pallas_call | solution.py:501
  164.6 1.3 reduce
  165.9 1.3 reduce.1
  167.2 3.2 %copy.70 = bf16[1024,1024]{1,0:T(8,128)(2,1)} copy(bf16[1024,1024]{1,0:T(8,128)(2,1)} %get-tuple-element.96) | data formatting | bytes 4194304
  170.4 1.3 copy.71
  171.7 0.1 copy-done.8
  171.8 0.8 copy.72
  172.6 0.8 copy.73
  173.4 0.8 copy.74
  174.2 0.0 copy-done.5
  174.2 0.0 copy-start.2
  174.2 0.8 copy.75
  175.0 0.8 copy.76
  175.8 0.8 copy.77
  176.6 0.0 copy-done.16
  176.6 0.0 copy-start.17
  176.6 0.7 copy.78
  177.3 0.0 copy-done.15
  177.3 0.7 copy.79
  177.9 0.0 copy-done.14
  177.9 0.7 copy.80
  178.6 0.7 copy.81
  179.2 0.5 copy.82
  179.8 0.5 copy.83
  180.3 0.8 copy.84
  181.1 0.8 copy.85
  181.9 0.7 copy.86
  182.5 0.7 copy.87
  183.2 0.7 copy.88
  183.8 0.7 copy.89
  184.5 0.5 copy.90
  185.0 0.5 copy.91
  (35 shorter events, 0.1 us)
Async XLA Ops:
  167.2 3.2 %copy-start = (bf16[1024,1024]{1,0:T(8,128)(2,1)S(1)}, bf16[1024,1024]{1,0:T(8,128)(2,1)}, u32[]{:S(2)}) copy-start(bf16[1024,1024]{1,0:T(8,128)(2,1)} %get-tuple-element.97) | copy-start | bytes 6291460
  170.4 1.4 copy-start.8
  170.4 2.2 %copy-start.7 = (bf16[1024,256]{1,0:T(8,128)(2,1)S(1)}, bf16[1024,256]{1,0:T(8,128)(2,1)}, u32[]{:S(2)}) copy-start(bf16[1024,256]{1,0:T(8,128)(2,1)} %get-tuple-element.99) | copy-start | bytes 1572868
  171.8 1.6 copy-start.6
  171.8 2.4 %copy-start.5 = (bf16[256,1024]{1,0:T(8,128)(2,1)S(1)}, bf16[256,1024]{1,0:T(8,128)(2,1)}, u32[]{:S(2)}) copy-start(bf16[256,1024]{1,0:T(8,128)(2,1)} %get-tuple-element.101) | copy-start | bytes 1572868
  171.8 3.2 %copy-start.4 = (f32[128,1024]{1,0:T(8,128)S(1)}, f32[128,1024]{1,0:T(8,128)}, u32[]{:S(2)}) copy-start(f32[128,1024]{1,0:T(8,128)} %get-tuple-element.104) | copy-start | bytes 1572868
  172.6 3.2 %copy-start.3 = (f32[1024,128]{1,0:T(8,128)S(1)}, f32[1024,128]{1,0:T(8,128)}, u32[]{:S(2)}) copy-start(f32[1024,128]{1,0:T(8,128)} %get-tuple-element.105) | copy-start | bytes 1572868
  173.4 3.2 %copy-start.16 = (f32[128,256]{1,0:T(8,128)S(1)}, f32[128,256]{1,0:T(8,128)}, u32[]{:S(2)}) copy-start(f32[128,256]{1,0:T(8,128)} %get-tuple-element.106) | copy-start | bytes 393220
  173.4 3.9 %copy-start.15 = (f32[128,256]{1,0:T(8,128)S(1)}, f32[128,256]{1,0:T(8,128)}, u32[]{:S(2)}) copy-start(f32[128,256]{1,0:T(8,128)} %get-tuple-element.107) | copy-start | bytes 393220
  173.4 4.6 %copy-start.14 = (f32[128,256]{1,0:T(8,128)S(1)}, f32[128,256]{1,0:T(8,128)}, u32[]{:S(2)}) copy-start(f32[128,256]{1,0:T(8,128)} %get-tuple-element.108) | copy-start | bytes 393220
  174.2 4.4 %copy-start.13 = (f32[256,128]{1,0:T(8,128)S(1)}, f32[256,128]{1,0:T(8,128)}, u32[]{:S(2)}) copy-start(f32[256,128]{1,0:T(8,128)} %get-tuple-element.109) | copy-start | bytes 393220
  174.2 5.1 %copy-start.20 = (f32[1,128]{1,0:T(1,128)S(1)}, f32[1,128]{1,0:T(1,128)}, u32[]{:S(2)}) copy-start(f32[1,128]{1,0:T(1,128)} %get-tuple-element.62) | copy-start | bytes 1540
  174.2 5.6 %copy-start.19 = (f32[1,128]{1,0:T(1,128)S(1)}, f32[1,128]{1,0:T(1,128)}, u32[]{:S(2)}) copy-start(f32[1,128]{1,0:T(1,128)} %get-tuple-element.63) | copy-start | bytes 1540
  174.2 6.1 %copy-start.2 = (f32[128,1024]{1,0:T(8,128)S(1)}, f32[128,1024]{1,0:T(8,128)}, u32[]{:S(2)}) copy-start(f32[128,1024]{1,0:T(8,128)} %get-tuple-element.112) | copy-start | bytes 1572868
  175.0 6.1 %copy-start.1 = (f32[1024,128]{1,0:T(8,128)S(1)}, f32[1024,128]{1,0:T(8,128)}, u32[]{:S(2)}) copy-start(f32[1024,128]{1,0:T(8,128)} %get-tuple-element.113) | copy-start | bytes 1572868
  175.8 6.1 %copy-start.12 = (f32[128,256]{1,0:T(8,128)S(1)}, f32[128,256]{1,0:T(8,128)}, u32[]{:S(2)}) copy-start(f32[128,256]{1,0:T(8,128)} %get-tuple-element.114) | copy-start | bytes 393220
  175.8 6.7 %copy-start.11 = (f32[128,256]{1,0:T(8,128)S(1)}, f32[128,256]{1,0:T(8,128)}, u32[]{:S(2)}) copy-start(f32[128,256]{1,0:T(8,128)} %get-tuple-element.115) | copy-start | bytes 393220
  176.6 6.6 %copy-start.10 = (f32[128,256]{1,0:T(8,128)S(1)}, f32[128,256]{1,0:T(8,128)}, u32[]{:S(2)}) copy-start(f32[128,256]{1,0:T(8,128)} %get-tuple-element.116) | copy-start | bytes 393220
  176.6 7.2 %copy-start.9 = (f32[256,128]{1,0:T(8,128)S(1)}, f32[256,128]{1,0:T(8,128)}, u32[]{:S(2)}) copy-start(f32[256,128]{1,0:T(8,128)} %get-tuple-element.117) | copy-start | bytes 393220
  176.6 7.9 %copy-start.18 = (f32[1,128]{1,0:T(1,128)S(1)}, f32[1,128]{1,0:T(1,128)}, u32[]{:S(2)}) copy-start(f32[1,128]{1,0:T(1,128)} %get-tuple-element.70) | copy-start | bytes 1540
  176.6 8.4 %copy-start.17 = (f32[1,128]{1,0:T(1,128)S(1)}, f32[1,128]{1,0:T(1,128)}, u32[]{:S(2)}) copy-start(f32[1,128]{1,0:T(1,128)} %get-tuple-element.71) | copy-start | bytes 1540

commit v2 on v1

--- a/solution.py
+++ b/solution.py
@@ -30,26 +30,68 @@
 ORDER = ((1, 1), (0, 1), (1, 0), (0, 0))
 
 
+def place_of(r, k2, k1, ky):
+    bit = lambda v, k: v if k == 0 else 1 - v
+    return (bit(r // 4, k2) * 2 + bit((r // 2) % 2, k1)) * 2 + bit(r % 2, ky)
+
+
+def slab_of(shapes, r, g, b, ref):
+    at = place_of(r, b // 4, (b // 2) % 2, b % 2)
+    h, w = shapes[g]
+    if GROUPS[g].rows:
+        return ref.at[pl.ds(pl.multiple_of(at * h, h), h), :]
+    return ref.at[:, pl.ds(pl.multiple_of(at * w, w), w)]
+
+
+def lanes_of(shapes, g, ref, i):
+    n = len(GROUPS[g].members)
+    w = shapes[g][1] // n
+    return ref if n == 1 else ref.at[:, i * w : (i + 1) * w]
+
+
+def finish(shapes, *refs):
+    n = len(GROUPS)
+    full, own, st = refs[0:n], refs[n : 2 * n], refs[2 * n : 3 * n]
+    vectors = refs[3 * n : 3 * n + 6]
+    halves, nexts, news = (refs[3 * n + 6 + 8 * k : 3 * n + 14 + 8 * k] for k in range(3))
+    sem, vec_sem = refs[3 * n + 30 :]
+    r = lax.axis_index("replica")
+    for g, group in enumerate(GROUPS):
+        for i, a in enumerate(group.members):
+            for b in range(8):
+                src = lanes_of(shapes, g, full[g].at[b], i)
+                pltpu.make_async_copy(src, slab_of(shapes, r, g, b, halves[a]), sem.at[0, g]).start()
+            pltpu.make_async_copy(lanes_of(shapes, g, own[g], i), nexts[a], sem.at[1, g]).start()
+            pltpu.make_async_copy(lanes_of(shapes, g, st[g], i), news[a], sem.at[2, g]).start()
+    copies = []
+    for i, dst in enumerate((*halves[6:], *nexts[6:], *news[6:])):
+        copies.append(pltpu.make_async_copy(vectors[i], dst, vec_sem.at[i]))
+        copies[-1].start()
+    for g in range(n):
+        for k, ref in enumerate((full[g], own[g], st[g])):
+            pltpu.make_async_copy(ref, ref, sem.at[k, g]).wait()
+    for c in copies:
+        c.wait()
+
+
 def kernel(replicas, models, limit, shapes, *refs):
     slopes, slope_norm, slope_bias = refs[0:6], refs[6], refs[7]
     params, param_norm, param_bias = refs[8:14], refs[14], refs[15]
     states, state_norm, state_bias = refs[16:22], refs[22], refs[23]
-    halves, half_norm, half_bias = refs[24:30], refs[30], refs[31]
-    nexts, next_norm, next_bias = refs[32:38], refs[38], refs[39]
-    news, new_norm, new_bias = refs[40:46], refs[46], refs[47]
-    scratch = list(refs[48:])
     groups = range(len(GROUPS))
+    n = len(GROUPS)
+    full, own, st = refs[24 : 24 + n], refs[24 + n : 24 + 2 * n], refs[24 + 2 * n : 24 + 3 * n]
+    half_norm, half_bias, next_norm, next_bias, new_norm, new_bias = refs[24 + 3 * n : 30 + 3 * n]
+    scratch = list(refs[30 + 3 * n :])
     take = lambda: [scratch.pop(0) for _ in groups]
-    xin, enc1, rec1, enc2, rec2, enc3, rec3, own, st, full, sq, sqr = (take() for _ in range(12))
-    vs, vown, vrec, vnext, vag = (scratch.pop(0) for _ in range(5))
+    xin, enc1, rec1, enc2, rec2, enc3, rec3, sq, sqr = (take() for _ in range(9))
+    vs, vown, vrec, vnext, vag, vh_norm, vh_bias = (scratch.pop(0) for _ in range(7))
     rs_s, rs_r, ag_s, ag_r, n_s, n_r, v_s, v_r, w_s, w_r = (scratch.pop(0) for _ in range(10))
-    load_sem, own_sem, st_sem, half_sem, next_sem, new_sem, vown_sem = scratch
+    load_sem, own_sem, st_sem, vown_sem = scratch
 
     r = lax.axis_index("replica")
     m = lax.axis_index("model")
-    far, near, y = r // 4, (r // 2) % 2, r % 2
-    bit = lambda v, k: v if k == 0 else 1 - v
-    place = lambda k2, k1, ky: (bit(far, k2) * 2 + bit(near, k1)) * 2 + bit(y, ky)
+    place = functools.partial(place_of, r)
     y_peer, near_peer, far_peer = place(0, 0, 1), place(0, 1, 0), place(1, 0, 0)
 
     scale = 2.0**13 / (limit * replicas)
@@ -69,17 +111,8 @@
     def block(g, kf, ks, kt):
         return kt * 4 + (kf * 2 + ks if GROUPS[g].near_first else ks * 2 + kf)
 
-    def slab(g, b, ref, i):
-        at = place(b // 4, (b // 2) % 2, b % 2)
-        h, w = shapes[g]
-        if GROUPS[g].rows:
-            return ref.at[pl.ds(pl.multiple_of(at * h, h), h), :]
-        return ref.at[:, pl.ds(pl.multiple_of(at * w, w), w)]
-
-    def lanes(g, ref, i):
-        n = len(GROUPS[g].members)
-        w = shapes[g][1] // n
-        return ref if n == 1 else ref.at[:, i * w : (i + 1) * w]
+    lanes = functools.partial(lanes_of, shapes)
+    slab = lambda g, b, ref, i: slab_of(shapes, r, g, b, ref)
 
     def loop(g, body):
         h, w = shapes[g]
@@ -279,14 +312,6 @@
 
             loop(g, body)
         gather3(g).start()
-        put(g, 0)
-        for i, a in enumerate(GROUPS[g].members):
-            pltpu.make_async_copy(lanes(g, own[g], i), nexts[a], next_sem.at[g]).start()
-            pltpu.make_async_copy(lanes(g, st[g], i), news[a], new_sem.at[g]).start()
-
-    def put(g, b):
-        for i, a in enumerate(GROUPS[g].members):
-            pltpu.make_async_copy(lanes(g, full[g].at[b], i), slab(g, b, halves[a], i), half_sem.at[g]).start()
 
     def gather3(g):
         return remote(
@@ -320,17 +345,14 @@
         gather3(g).wait_recv()
         gather2(g, 1).start()
         gather1(g, 1, 0).start()
-        put(g, block(g, 0, 0, 1))
 
     def got2(g, kt):
         gather2(g, kt).wait_recv()
         gather1(g, kt, 1).start()
-        put(g, block(g, 0, 1, kt))
 
     def got1(g):
         for kt, ks in ((0, 0), (1, 0), (0, 1), (1, 1)):
             gather1(g, kt, ks).wait_recv()
-            put(g, block(g, 1, ks, kt))
 
     width = vs.shape[1] // replicas
 
@@ -363,13 +385,15 @@
             vec_back(j).start()
 
     def vec_finish():
-        half_norm[r] = vnext[0:1, :].astype(jnp.bfloat16)
-        half_bias[r] = vnext[1:2, :].astype(jnp.bfloat16)
+        vh_norm[pl.ds(r, 1), :] = vnext[0:1, :]
+        vh_bias[pl.ds(r, 1), :] = vnext[1:2, :]
         for j in range(1, replicas):
             vec_back(j).wait_recv()
             at = lax.rem(r + replicas - j, replicas)
-            half_norm[at] = vag[j - 1, 0:1, :].astype(jnp.bfloat16)
-            half_bias[at] = vag[j - 1, 1:2, :].astype(jnp.bfloat16)
+            vh_norm[pl.ds(at, 1), :] = vag[j - 1, 0:1, :]
+            vh_bias[pl.ds(at, 1), :] = vag[j - 1, 1:2, :]
+        half_norm[...] = vh_norm[...].astype(jnp.bfloat16)
+        half_bias[...] = vh_bias[...].astype(jnp.bfloat16)
 
     vs[0:1, :] = slope_norm[...]
     vs[1:2, :] = slope_bias[...]
@@ -456,9 +480,6 @@
         gather3(g).wait_send()
         for j in range(1, models):
             copyn(g, j).wait_send()
-        pltpu.make_async_copy(full[g], full[g], half_sem.at[g]).wait()
-        pltpu.make_async_copy(own[g], own[g], next_sem.at[g]).wait()
-        pltpu.make_async_copy(st[g], st[g], new_sem.at[g]).wait()
     for j in range(1, replicas):
         vec_out(j).wait_send()
         vec_back(j).wait_send()
@@ -476,13 +497,13 @@
         h, w = params[g.members[0]].shape
         shapes.append((h, w * len(g.members)))
     S = jax.ShapeDtypeStruct
-    outs = [S(a.shape[1:], bf16) for a in slopes] + [S((replicas, 1, width), bf16)] * 2
-    for _ in range(2):
-        outs += [S(a.shape, f32) for a in params] + [S((1, width), f32)] * 2
+    n = len(GROUPS)
+    held = [((replicas, *s), bf16) for s in shapes] + [(s, f32) for s in shapes] * 2
+    held += [((replicas, width), bf16)] * 2 + [((1, width), f32)] * 4
     ANY, VM = pl.BlockSpec(memory_space=pl.ANY), pl.BlockSpec(memory_space=pltpu.VMEM)
     part = [ANY] * 6 + [VM] * 2
     scratch = []
-    for count, dtype in ((8, f32), (4, bf16), (4, bf16), (2, bf16), (2, bf16), (0, bf16), (0, bf16), (0, f32), (0, f32), (8, bf16)):
+    for count, dtype in ((8, f32), (4, bf16), (4, bf16), (2, bf16), (2, bf16), (0, bf16), (0, bf16)):
         scratch += [pltpu.VMEM((count, *s) if count else s, dtype) for s in shapes]
     sq = [(2, len(g.members), s[0], 128) if g.rows else (2, 8, s[1]) for g, s in zip(GROUPS, shapes)]
     scratch += [pltpu.VMEM(s, f32) for s in sq]
@@ -493,21 +514,33 @@
         pltpu.VMEM((replicas - 1, 2, width), f32),
         pltpu.VMEM((2, width), f32),
         pltpu.VMEM((replicas - 1, 2, width), f32),
+        pltpu.VMEM((replicas, width), f32),
+        pltpu.VMEM((replicas, width), f32),
     ]
     dma = pltpu.SemaphoreType.DMA
-    n = len(GROUPS)
     scratch += [dma((n, 7))] * 4 + [dma((n, models - 1))] * 2 + [dma((replicas - 1,))] * 4
-    scratch += [dma((n, 8))] + [dma((n,))] * 5 + [dma(())]
+    scratch += [dma((n, 8))] + [dma((n,))] * 2 + [dma(())]
     out = pl.pallas_call(
         functools.partial(kernel, replicas, models, 4.0, shapes),
-        out_shape=outs,
+        out_shape=[pltpu.VMEM(*h) for h in held],
         in_specs=part * 3,
-        out_specs=part * 3,
+        out_specs=[VM] * len(held),
         scratch_shapes=scratch,
         compiler_params=pltpu.CompilerParams(
-            collective_id=0, has_side_effects=True, vmem_limit_bytes=60 * 1024 * 1024
+            collective_id=0, has_side_effects=True, vmem_limit_bytes=54 * 1024 * 1024
         ),
     )(*args)
+    outs = [S(a.shape[1:], bf16) for a in slopes] + [S((replicas, width), bf16)] * 2
+    for _ in range(2):
+        outs += [S(a.shape, f32) for a in params] + [S((1, width), f32)] * 2
+    out = pl.pallas_call(
+        functools.partial(finish, shapes),
+        out_shape=outs,
+        in_specs=[VM] * len(held),
+        out_specs=[ANY] * len(outs),
+        scratch_shapes=[dma((3, n)), dma((6,))],
+        compiler_params=pltpu.CompilerParams(vmem_limit_bytes=1024 * 1024),
+    )(*out)
     flat = lambda a: a.reshape(-1)
     return (
         *out[0:6], flat(out[6]), flat(out[7]),

time: 186 us -> 167 us (0.90)
  local copies, waits for them, and re-layouts: 18.3 us -> 0 us
  other arithmetic: 2.56 us -> 0 us
  Pallas kernels: 164 us -> 166 us
    unnamed x64 -> x0, local copies, waits for them, and re-layouts: 18.3 us -> none
    pallas_call x0 -> x1, Pallas kernels: none -> 3.8 us  [fused(): pl.pallas_call(functools.partial(finish, shapes), out_shape=outs, in_spec...]
    pallas_call x2 -> x0, other arithmetic: 2.56 us -> none  [fused(): pl.pallas_call(functools.partial(kernel, replicas, models, 4.0, shapes),...]
where the time goes in v2:
time: 167 us
  Pallas kernels  166 us (99%)
    pallas_call x1, Pallas kernels, fused(): pl.pallas_call(functools.partial(kernel, replicas, models, 4.0, shapes),...  163 us
    pallas_call x1, Pallas kernels, fused(): pl.pallas_call(functools.partial(finish, shapes), out_shape=outs, in_spec...  3.8 us

profile of v2, /device:TPU:10, one launch (start us, length us, event | category | flops | bytes accessed | tf_op | source)
XLA Modules:
  0.0 167.1 jit_solution(16403981624551660007)
XLA Ops:
  0.7 162.6 %shard_map.415 = (bf16[8,128,1024]{2,1,0:T(8,128)(2,1)S(1)}, bf16[8,1024,128]{2,1,0:T(8,128)(2,1)S(1)}, bf16[8,256,128]{2,1,0:T(8,128)(2,1)S(1)}, bf16[8,128,768...) custom-call(f32[1,1024,1024]{2,1,0:T(8,128)} %refs_0_.1, ...), custom_call_target="tpu_custom_call" | custom-call | tf_op jit(solution)/shard_map/pallas_call | solution.py:523
  163.3 3.8 %shard_map.416 = (bf16[1024,1024]{1,0:T(8,128)(2,1)}, bf16[1024,1024]{1,0:T(8,128)(2,1)}, bf16[1024,256]{1,0:T(8,128)(2,1)}, bf16[1024,256]{1,0:T(8,128)(2,1)}, ...) custom-call(bf16[8,128,1024]{2,1,0:T(8,128)(2,1)S(1)} %get-tuple-ele, ...), custom_call_target="tpu_custom_call" | custom-call | tf_op jit(solution)/shard_map/pallas_call | solution.py:536
